TPU v7x, 256 devices: a whole 4x4x8 slice. The times are simulated.
256 devices in a mesh: ex: 16 (over y, x_lo, core), tp: 16 (over x_hi, z).
Axes of the slice: x: 4 (x_hi: 2, x_lo: 2; x = x_hi * 2 + x_lo), y: 4, z: 8, core: 2. Of those that a mesh axis runs over, the one named last changes fastest.
Arguments:
- samples: bfloat16 [1536, 2048], P(('ex', 'tp')), may hold values from -6 to 6
- gate_weight: bfloat16 [2048, 44], replicated, may hold values from -15 to 15
- up_weight: bfloat16 [16, 2048, 4096], P('ex', None, 'tp'), may hold values from -0.125 to 0.125
- down_weight: bfloat16 [16, 4096, 2048], P('ex', 'tp'), may hold values from -0.09375 to 0.09375
Outputs:
- task_outputs: bfloat16 [1536, 5, 2048], P(('ex', 'tp'))
All inputs are finite; a program needn't handle non-finite values.
Results may differ from a plain program's by a relative error of at most 0.0055.
Values may be sent and summed in bfloat16 or wider, within the bound.
No kernel may reach another device: no remote copies, remote signals or barrier semaphores. Data moves between devices by JAX's collectives and lax.ppermute only.
A program may use at most 128 MiB of HBM per device.

v0:
```python
import jax
import jax.numpy as jnp
import numpy as np
from jax import lax
from jax.sharding import Mesh
from jax.sharding import PartitionSpec as P

TASKS = 4
TASK_EXP = 3
SHARED = 4
EXPERTS = 16
GATES = 44
TP = ("tp_0", "tp_1")
EX_TP = ("ex", "tp_0", "tp_1")


def own_block(pieces, axes, order):
    shape = [lax.axis_size(a) for a in axes]
    pieces = pieces.reshape(*shape, *pieces.shape[1:])
    pieces = pieces.transpose(*order, *range(len(axes), pieces.ndim))
    pieces = pieces.reshape(-1, *pieces.shape[len(axes) :])
    for k in order:
        pieces = lax.psum_scatter(pieces, axes[k], scatter_dimension=0, tiled=True)
    return pieces[0]


def cut_along(shard, dim, devices):
    shape = shard.shape
    pieces = shard.reshape(*shape[:dim], devices, shape[dim] // devices, *shape[dim + 1 :])
    return jnp.moveaxis(pieces, dim, 0)


def sum_by_axis(shard, axes, order, dim):
    devices = lax.axis_size(axes)
    return own_block(cut_along(shard, dim, devices), axes, order)


def routing_table():
    per_task = TASK_EXP + SHARED
    table = np.zeros((GATES, (TASKS + 1) * EXPERTS), np.float32)
    for task_idx in range(TASKS):
        for column in range(per_task):
            if column < TASK_EXP:
                expert_idx = task_idx * TASK_EXP + column
            else:
                expert_idx = TASKS * TASK_EXP + column - TASK_EXP
            table[task_idx * per_task + column, task_idx * EXPERTS + expert_idx] = 1.0
    for expert_idx in range(EXPERTS):
        table[TASKS * per_task + expert_idx, TASKS * EXPERTS + expert_idx] = 1.0
    return jnp.asarray(table, dtype=jnp.float32)


def gate_mix(rows, gate_weight):
    logits = jnp.dot(rows, gate_weight, preferred_element_type=jnp.float32)
    per_task = TASK_EXP + SHARED
    pieces = []
    for task_idx in range(TASKS):
        pieces.append(
            jax.nn.softmax(logits[:, task_idx * per_task : (task_idx + 1) * per_task], axis=-1)
        )
    pieces.append(jax.nn.softmax(logits[:, TASKS * per_task :], axis=-1))
    probs = jnp.concatenate(pieces, axis=1)
    mixed = jnp.dot(probs, routing_table(), precision=lax.Precision.HIGHEST)
    return mixed.reshape(rows.shape[0], TASKS + 1, EXPERTS)


def on_device(samples, gate_weight, up_weight, down_weight):
    local_experts = up_weight.shape[0]
    ex_count = lax.axis_size("ex")
    tp_count = lax.axis_size(TP)
    row_dev = samples.shape[0]
    width = samples.shape[1]
    outputs = [
        jnp.maximum(
            jnp.dot(
                lax.all_gather(samples, EX_TP, axis=0, tiled=True),
                up_weight[0],
                preferred_element_type=jnp.float32,
            ),
            0.0,
        ).astype(jnp.bfloat16)
    ]
    hidden = jnp.stack(outputs, axis=1)
    partial_out = jnp.einsum(
        "rlf,lfd->rld", hidden, down_weight, preferred_element_type=jnp.float32
    )
    blocked = partial_out.reshape(ex_count, tp_count * row_dev, local_experts, width)
    summed = sum_by_axis(blocked, TP, (1, 0), 1)
    gathered = lax.all_to_all(summed, "ex", split_axis=0, concat_axis=2, tiled=True)[0]
    mixing = gate_mix(samples, gate_weight)
    result = jnp.einsum("rke,red->rkd", mixing, gathered, precision=lax.Precision.HIGHEST)
    return result.astype(jnp.bfloat16)


def solution(mesh):
    torus = Mesh(mesh.devices.reshape(mesh.shape["ex"], 2, 8), ("ex", "tp_0", "tp_1"))
    return jax.shard_map(
        on_device,
        mesh=torus,
        in_specs=(P(EX_TP, None), P(), P("ex", None, TP), P("ex", TP, None)),
        out_specs=P(EX_TP, None, None),
        check_vma=False,
    )
```

profile of v0, /device:TPU:1, one launch (start us, length us, event | category | flops | bytes accessed | tf_op | source)
XLA Modules:
  0.0 1006.1 jit_solution(12490226388472743928)
XLA Ops:
  6.5 0.7 all-gather.3.cloned.1.call-update
  7.3 0.0 reduce-scatter.3.cloned.1.call-start
  7.3 727.8 %all-gather.3.cloned.1.call-done = bf16[256,6,2048]{2,1,0:T(8,128)(2,1)} async-done(((bf16[1,6,2048]{2,1,0:T(8,128)(2,1)}), bf16[256,6,2048]{2,1,0:T(8,128)(2,1)}) %all-gather.3.cloned.1.call-update) | async-done | bytes 6291472 | tf_op jit(solution)/shard_map/all_gather | solution.py:76
  735.1 11.1 %reshape.31 = bf16[1536,2048]{1,0:T(8,128)(2,1)} reshape(bf16[256,6,2048]{2,1,0:T(8,128)(2,1)} %all-gather.3.cloned.1.call-done) | data formatting | bytes 12582912
  746.2 13.8 %convolution_bitcast_fusion = f32[1536,1,2048]{2,0,1:T(8,128)} fusion(bf16[1,256,2048]{2,1,0:T(8,128)(2,1)S(1)} %copy-done, bf16[1536,2048]{1,0:T(8,128)(2,1)} %reshape.31, bf16[1,2048,256]{2,1,0:T(8,128)(2,1)S(1)} %copy-done.2), kind=kOutput, calls=%fused_computation | convolution fusion | flops 3222011904 | bytes 20971520 | tf_op jit(solution)/shard_map/rlf,lfd->rld/dot_general | solution.py:84
  759.9 19.3 %reshape_reshape.3 = f32[16,16,6,1,2048]{4,3,2,1,0:T(1,128)} reshape(f32[1536,1,2048]{2,0,1:T(8,128)} %convolution_bitcast_fusion) | data formatting | bytes 25165824 | tf_op jit(solution)/shard_map/reshape;reshape | solution.py:29
  779.3 18.9 %copy.21 = f32[16,16,6,1,2048]{4,1,3,2,0:T(8,128)} copy(f32[16,16,6,1,2048]{4,3,2,0,1:T(1,128)} %bitcast.40) | data formatting | bytes 25165824 | tf_op jit(solution)/shard_map/transpose | solution.py:30
  798.1 11.2 %copy.22 = f32[8,2,16,6,1,2048]{5,2,4,3,1,0:T(8,128)} copy(f32[8,2,16,6,1,2048]{5,2,4,3,0,1:T(8,128)} %bitcast.41) | data formatting | bytes 25165824 | tf_op jit(solution)/shard_map/transpose | solution.py:20
  809.4 0.0 copy-start.7
  809.4 0.0 copy-start.6
  809.4 0.0 copy-start.5
  809.4 0.0 reduce-scatter.3.cloned.1.call-update
  809.4 0.3 reduce-scatter.5.cloned.1.call-start
  809.7 133.9 %reduce-scatter.3.cloned.1.call-done = f32[2,16,6,1,2048]{4,1,3,2,0:T(8,128)} async-done(((f32[16,16,6,1,2048]{4,1,3,2,0:T(8,128)}), f32[2,16,6,1,2048]{4,1,3,2,0:T(8,128)}) %reduce-scatter.3.cloned.1.call-update) | async-done | bytes 1572880 | tf_op jit(solution)/shard_map/reduce_scatter | solution.py:23
  943.6 0.0 reduce-scatter.5.cloned.1.call-update
  943.6 0.2 fusion.29
  943.8 0.2 slice_reduce_fusion
  944.0 0.2 slice_reduce_fusion.1
  944.2 0.2 fusion.16
  944.4 0.2 fusion.10
  944.6 0.2 convolution_add_fusion.3
  944.9 32.5 %reduce-scatter.5.cloned.1.call-done = f32[1,16,6,1,2048]{4,1,3,2,0:T(8,128)} async-done(((f32[2,16,6,1,2048]{4,1,3,2,0:T(8,128)}), f32[1,16,6,1,2048]{4,1,3,2,0:T(8,128)}) %reduce-scatter.5.cloned.1.call-update) | async-done | bytes 786448 | tf_op jit(solution)/shard_map/reduce_scatter | solution.py:23
  977.4 2.8 copy.23
  980.2 5.1 all-to-all-start
  985.3 0.2 fusion.17
  985.5 0.2 convolution_add_fusion.2
  985.7 0.2 convolution_add_fusion.1
  986.0 0.2 convolution_add_fusion
  986.2 0.1 reshape.26
  986.3 11.6 %all-to-all-done = f32[16,6,1,2048]{3,2,1,0:T(1,128)S(1)} async-done(((f32[16,6,1,2048]{3,2,1,0:T(1,128)}), f32[16,6,1,2048]{3,2,1,0:T(1,128)S(1)}, u32[]{:S(2)}, u32[]{:S(2)}) %all-to-all-start) | async-done | bytes 786464 | tf_op jit(solution)/shard_map/all_to_all | solution.py:89
  997.9 0.9 convolution_convert_fusion
  998.8 0.8 copy.25
  (18 shorter events, 0.0 us)
Async XLA Ops:
  6.5 739.7 %copy-start = (bf16[1,256,2048]{2,1,0:T(8,128)(2,1)S(1)}, bf16[1,256,2048]{2,1,0:T(8,128)(2,1)}, u32[]{:S(2)}) copy-start(bf16[1,256,2048]{2,1,0:T(8,128)(2,1)} %param.8) | copy-start | bytes 3145732
  6.5 728.6 %all-gather.3.cloned.1.call-start = ((), (), s32[]{:S(2)}) async-start(), calls=%async_computation.5 | async-start | bytes 8421376 | tf_op jit(solution)/shard_map/all_gather | solution.py:76
  7.3 738.9 %copy-start.2 = (bf16[1,2048,256]{2,1,0:T(8,128)(2,1)S(1)}, bf16[1,2048,256]{2,1,0:T(8,128)(2,1)}, u32[]{:S(2)}) copy-start(bf16[1,2048,256]{2,1,0:T(8,128)(2,1)} %param.7) | copy-start | bytes 3145732
  7.3 936.3 %reduce-scatter.3.cloned.1.call-start = ((), (), s32[]{:S(2)}) async-start(), calls=%async_computation.3 | async-start | bytes 14155776 | tf_op jit(solution)/shard_map/reduce_scatter | solution.py:23
  809.4 134.3 %copy-start.3 = (bf16[2048,44]{0,1:T(8,128)(2,1)S(1)}, bf16[2048,44]{0,1:T(8,128)(2,1)}, u32[]{:S(2)}) copy-start(bf16[2048,44]{0,1:T(8,128)(2,1)} %param.6) | copy-start | bytes 540676
  809.4 134.3 %copy-start.4 = (bf16[6,2048]{1,0:T(8,128)(2,1)S(1)}, bf16[6,2048]{1,0:T(8,128)(2,1)}, u32[]{:S(2)}) copy-start(bf16[6,2048]{1,0:T(8,128)(2,1)} %param.5) | copy-start | bytes 73732
  809.4 135.1 %copy-start.8 = (f32[7,80]{1,0:T(8,128)S(1)}, f32[7,80]{1,0:T(8,128)}, u32[]{:S(2)}) copy-start(f32[7,80]{1,0:T(8,128)} %constant.12) | copy-start | bytes 6724
  809.4 135.3 %copy-start.9 = (f32[7,80]{1,0:T(8,128)S(1)}, f32[7,80]{1,0:T(8,128)}, u32[]{:S(2)}) copy-start(f32[7,80]{1,0:T(8,128)} %constant.13) | copy-start | bytes 6724
  809.4 176.2 %copy-start.7 = (f32[7,80]{1,0:T(8,128)S(1)}, f32[7,80]{1,0:T(8,128)}, u32[]{:S(2)}) copy-start(f32[7,80]{1,0:T(8,128)} %constant.14) | copy-start | bytes 6724
  809.4 176.4 %copy-start.6 = (f32[7,80]{1,0:T(8,128)S(1)}, f32[7,80]{1,0:T(8,128)}, u32[]{:S(2)}) copy-start(f32[7,80]{1,0:T(8,128)} %constant.15) | copy-start | bytes 6724
  809.4 176.6 %copy-start.5 = (f32[16,80]{1,0:T(8,128)S(1)}, f32[16,80]{1,0:T(8,128)}, u32[]{:S(2)}) copy-start(f32[16,80]{1,0:T(8,128)} %constant.16) | copy-start | bytes 15364
  809.4 190.2 %copy-start.1 = (bf16[1,256,2048]{2,1,0:T(8,128)(2,1)S(1)}, bf16[1,256,2048]{2,1,0:T(8,128)(2,1)}, u32[]{:S(2)}) copy-start(bf16[1,256,2048]{2,1,0:T(8,128)(2,1)} %param.8) | copy-start | bytes 3145732
  809.4 167.9 %reduce-scatter.5.cloned.1.call-start = ((), (), s32[]{:S(2)}) async-start(), calls=%async_computation.4 | async-start | bytes 2359296 | tf_op jit(solution)/shard_map/reduce_scatter | solution.py:23
  980.2 17.7 %all-to-all-start = ((f32[16,6,1,2048]{3,2,1,0:T(1,128)}), f32[16,6,1,2048]{3,2,1,0:T(1,128)S(1)}, u32[]{:S(2)}, u32[]{:S(2)}) async-start(f32[16,6,1,2048]{3,2,1,0:T(1,128)} %copy.23), calls=%async_computation.2 | async-start | bytes 1572864 | tf_op jit(solution)/shard_map/all_to_all | solution.py:89
Sparse Core Ops, SparseCore 0:
  9.2 725.8 all-gather.2
  809.5 133.9 reduce-scatter.2
  946.1 31.2 reduce-scatter.4
where the time goes:
time: 1010 us
  waiting for transfers between devices  907 us (90%)
  local copies, waits for them, and re-layouts  64.2 us (6%)
  matrix products  15.9 us (2%)
  between operations  13.2 us (1%)
    all_gather x1, waiting for transfers between devices, on_device(): lax.all_gather(samples, EX_TP, axis=0, tiled=True)  728 us
    reduce_scatter x2, waiting for transfers between devices, own_block(): pieces = lax.psum_scatter(pieces, axes[k], scatter_dimension=0, tiled=True)  166 us
  transfers between devices with their start and end apart: 4, of which 4 were waited for; matrix products, arithmetic and copies ran while one was open for 0% of the time, Pallas kernels for 0%

commit v1 on v0

--- a/solution.py
+++ b/solution.py
@@ -73,7 +73,9 @@
     outputs = [
         jnp.maximum(
             jnp.dot(
-                lax.all_gather(samples, EX_TP, axis=0, tiled=True),
+                jnp.concatenate(
+                    lax.all_to_all(jnp.stack([samples] * lax.axis_size(EX_TP)), EX_TP, 0, 0), axis=0
+                ),
                 up_weight[0],
                 preferred_element_type=jnp.float32,
             ),

time: 1010 us -> 480 us (0.48)
  waiting for transfers between devices: 907 us -> 174 us
  blocking collectives: 0 us -> 202 us
    all_gather x1 -> x0, waiting for transfers between devices: 728 us -> none  [on_device(): lax.all_gather(samples, EX_TP, axis=0, tiled=True)]
    all_to_all x0 -> x1, blocking collectives: none -> 202 us  [on_device(): lax.all_to_all(jnp.stack([samples] * lax.axis_size(EX_TP)), EX_TP, 0, 0)]
    reshape x0 -> x1, local copies, waits for them, and re-layouts: none -> 11.1 us  [on_device(): jnp.concatenate(lax.all_to_all(jnp.stack([samples] * lax.axis_size(EX_TP)...]
    unnamed x21 -> x20, local copies, waits for them, and re-layouts: 11.1 us -> 0.05 us
  transfers between devices with their start and end apart: 4 -> 3, of which waited for: 4 -> 3; matrix products, arithmetic and copies ran while one was open for 0% -> 0% of each run, Pallas kernels for 0% -> 0%
where the time goes in v1:
time: 480 us; the launch traced here: 478 us
  blocking collectives  202 us (42%)
  waiting for transfers between devices  174 us (36%)
  local copies, waits for them, and re-layouts  66.1 us (14%)
  matrix products  15.9 us (3%)
  between operations  13.5 us (3%)
  starting transfers between devices  5.42 us (1%)
    all_to_all x1, blocking collectives, on_device(): lax.all_to_all(jnp.stack([samples] * lax.axis_size(EX_TP)), EX_TP, 0, 0)  202 us
    reduce_scatter x2, waiting for transfers between devices, own_block(): pieces = lax.psum_scatter(pieces, axes[k], scatter_dimension=0, tiled=True)  163 us
    another operation x1, local copies, waits for them, and re-layouts, cut_along(): shard.reshape(*shape[:dim], devices, shape[dim] // devices, *shape[dim +...  19.3 us
    transpose x1, local copies, waits for them, and re-layouts, cut_along(): return jnp.moveaxis(pieces, dim, 0)  18.9 us
    dot_general x1, matrix products, on_device(): jnp.einsum('rlf,lfd->rld', hidden, down_weight, preferred_element_type=jn...  13.8 us
    all_to_all x1, waiting for transfers between devices, on_device(): lax.all_to_all(summed, 'ex', split_axis=0, concat_axis=2, tiled=True)[0]  11.6 us
    transpose x1, local copies, waits for them, and re-layouts, own_block(): pieces = pieces.transpose(*order, *range(len(axes), pieces.ndim))  11.2 us
    reshape x1, local copies, waits for them, and re-layouts, on_device(): jnp.concatenate(lax.all_to_all(jnp.stack([samples] * lax.axis_size(EX_TP)...  11.1 us
  transfers between devices with their start and end apart: 3, of which 3 were waited for; matrix products, arithmetic and copies ran while one was open for 0% of the time, Pallas kernels for 0%

profile of v1, /device:TPU:1, one launch (start us, length us, event | category | flops | bytes accessed | tf_op | source)
XLA Modules:
  0.0 478.5 jit_solution(10313420806770381599)
XLA Ops:
  6.5 1.9 stack.2
  8.4 202.4 %all_to_all.20 = bf16[256,6,2048]{2,1,0:T(8,128)(2,1)} all-to-all(bf16[256,6,2048]{2,1,0:T(8,128)(2,1)S(1)} %stack.2), channel_id=1, replica_groups=mesh['ex'=16,'tp_0'=2,'tp_1'=8] {'ex','tp_0','tp_1'}, dimensions={0} | all-to-all | bytes 12582912 | tf_op jit(solution)/shard_map/all_to_all | solution.py:77
  210.8 11.1 %reshape.32 = bf16[1536,2048]{1,0:T(8,128)(2,1)} reshape(bf16[256,6,2048]{2,1,0:T(8,128)(2,1)} %all_to_all.20) | data formatting | bytes 12582912 | tf_op jit(solution)/shard_map/reshape | solution.py:76
  222.0 13.8 %convolution_bitcast_fusion = f32[1536,1,2048]{2,0,1:T(8,128)} fusion(bf16[1,256,2048]{2,1,0:T(8,128)(2,1)S(1)} %copy-done, bf16[1536,2048]{1,0:T(8,128)(2,1)} %reshape.32, bf16[1,2048,256]{2,1,0:T(8,128)(2,1)S(1)} %copy-done.2), kind=kOutput, calls=%fused_computation | convolution fusion | flops 3222011904 | bytes 20971520 | tf_op jit(solution)/shard_map/rlf,lfd->rld/dot_general | solution.py:86
  235.7 19.3 %reshape_reshape.3 = f32[16,16,6,1,2048]{4,3,2,1,0:T(1,128)} reshape(f32[1536,1,2048]{2,0,1:T(8,128)} %convolution_bitcast_fusion) | data formatting | bytes 25165824 | tf_op jit(solution)/shard_map/reshape;reshape | solution.py:29
  255.0 18.9 %copy.21 = f32[16,16,6,1,2048]{4,1,3,2,0:T(8,128)} copy(f32[16,16,6,1,2048]{4,3,2,0,1:T(1,128)} %bitcast.39) | data formatting | bytes 25165824 | tf_op jit(solution)/shard_map/transpose | solution.py:30
  273.9 11.2 %copy.22 = f32[8,2,16,6,1,2048]{5,2,4,3,1,0:T(8,128)} copy(f32[8,2,16,6,1,2048]{5,2,4,3,0,1:T(8,128)} %bitcast.40) | data formatting | bytes 25165824 | tf_op jit(solution)/shard_map/transpose | solution.py:20
  285.1 0.0 copy-start.7
  285.1 0.0 copy-start.6
  285.2 0.0 copy-start.5
  285.2 0.0 reduce-scatter.3.cloned.1.call-update
  285.2 0.0 copy-start.1
  285.2 0.3 reduce-scatter.5.cloned.1.call-start
  285.5 130.2 %reduce-scatter.3.cloned.1.call-done = f32[2,16,6,1,2048]{4,1,3,2,0:T(8,128)} async-done(((f32[16,16,6,1,2048]{4,1,3,2,0:T(8,128)}), f32[2,16,6,1,2048]{4,1,3,2,0:T(8,128)}) %reduce-scatter.3.cloned.1.call-update) | async-done | bytes 1572880 | tf_op jit(solution)/shard_map/reduce_scatter | solution.py:23
  415.6 0.0 reduce-scatter.5.cloned.1.call-update
  415.7 0.2 fusion.29
  415.8 0.2 slice_reduce_fusion
  416.0 0.2 slice_reduce_fusion.1
  416.3 0.2 fusion.16
  416.5 0.2 fusion.10
  416.7 0.2 convolution_add_fusion.3
  416.9 32.5 %reduce-scatter.5.cloned.1.call-done = f32[1,16,6,1,2048]{4,1,3,2,0:T(8,128)} async-done(((f32[2,16,6,1,2048]{4,1,3,2,0:T(8,128)}), f32[1,16,6,1,2048]{4,1,3,2,0:T(8,128)}) %reduce-scatter.5.cloned.1.call-update) | async-done | bytes 786448 | tf_op jit(solution)/shard_map/reduce_scatter | solution.py:23
  449.4 2.8 copy.23
  452.3 5.2 %all-to-all-start.1 = ((f32[16,6,1,2048]{3,2,1,0:T(1,128)}), f32[16,6,1,2048]{3,2,1,0:T(1,128)S(1)}, u32[]{:S(2)}, u32[]{:S(2)}) async-start(f32[16,6,1,2048]{3,2,1,0:T(1,128)} %copy.23), calls=%async_computation.3 | async-start | bytes 1572864 | tf_op jit(solution)/shard_map/all_to_all | solution.py:91
  457.4 0.2 fusion.17
  457.6 0.2 convolution_add_fusion.2
  457.8 0.2 convolution_add_fusion.1
  458.0 0.2 convolution_add_fusion
  458.2 0.1 reshape.31
  458.3 11.6 %all-to-all-done.1 = f32[16,6,1,2048]{3,2,1,0:T(1,128)S(1)} async-done(((f32[16,6,1,2048]{3,2,1,0:T(1,128)}), f32[16,6,1,2048]{3,2,1,0:T(1,128)S(1)}, u32[]{:S(2)}, u32[]{:S(2)}) %all-to-all-start.1) | async-done | bytes 786464 | tf_op jit(solution)/shard_map/all_to_all | solution.py:91
  470.0 0.9 convolution_convert_fusion
  470.9 0.8 copy.25
  (17 shorter events, 0.0 us)
Async XLA Ops:
  6.5 215.4 %copy-start = (bf16[1,256,2048]{2,1,0:T(8,128)(2,1)S(1)}, bf16[1,256,2048]{2,1,0:T(8,128)(2,1)}, u32[]{:S(2)}) copy-start(bf16[1,256,2048]{2,1,0:T(8,128)(2,1)} %param.8) | copy-start | bytes 3145732
  6.5 409.1 %reduce-scatter.3.cloned.1.call-start = ((), (), s32[]{:S(2)}) async-start(), calls=%async_computation.4 | async-start | bytes 14155776 | tf_op jit(solution)/shard_map/reduce_scatter | solution.py:23
  210.8 11.1 %copy-start.2 = (bf16[1,2048,256]{2,1,0:T(8,128)(2,1)S(1)}, bf16[1,2048,256]{2,1,0:T(8,128)(2,1)}, u32[]{:S(2)}) copy-start(bf16[1,2048,256]{2,1,0:T(8,128)(2,1)} %param.7) | copy-start | bytes 3145732
  285.1 130.6 %copy-start.3 = (bf16[2048,44]{0,1:T(8,128)(2,1)S(1)}, bf16[2048,44]{0,1:T(8,128)(2,1)}, u32[]{:S(2)}) copy-start(bf16[2048,44]{0,1:T(8,128)(2,1)} %param.6) | copy-start | bytes 540676
  285.1 130.6 %copy-start.4 = (bf16[6,2048]{1,0:T(8,128)(2,1)S(1)}, bf16[6,2048]{1,0:T(8,128)(2,1)}, u32[]{:S(2)}) copy-start(bf16[6,2048]{1,0:T(8,128)(2,1)} %param.5) | copy-start | bytes 73732
  285.1 131.4 %copy-start.8 = (f32[7,80]{1,0:T(8,128)S(1)}, f32[7,80]{1,0:T(8,128)}, u32[]{:S(2)}) copy-start(f32[7,80]{1,0:T(8,128)} %constant.12) | copy-start | bytes 6724
  285.1 131.6 %copy-start.9 = (f32[7,80]{1,0:T(8,128)S(1)}, f32[7,80]{1,0:T(8,128)}, u32[]{:S(2)}) copy-start(f32[7,80]{1,0:T(8,128)} %constant.13) | copy-start | bytes 6724
  285.1 172.5 %copy-start.7 = (f32[7,80]{1,0:T(8,128)S(1)}, f32[7,80]{1,0:T(8,128)}, u32[]{:S(2)}) copy-start(f32[7,80]{1,0:T(8,128)} %constant.14) | copy-start | bytes 6724
  285.1 172.7 %copy-start.6 = (f32[7,80]{1,0:T(8,128)S(1)}, f32[7,80]{1,0:T(8,128)}, u32[]{:S(2)}) copy-start(f32[7,80]{1,0:T(8,128)} %constant.15) | copy-start | bytes 6724
  285.2 172.9 %copy-start.5 = (f32[16,80]{1,0:T(8,128)S(1)}, f32[16,80]{1,0:T(8,128)}, u32[]{:S(2)}) copy-start(f32[16,80]{1,0:T(8,128)} %constant.16) | copy-start | bytes 15364
  285.2 186.5 %copy-start.1 = (bf16[1,256,2048]{2,1,0:T(8,128)(2,1)S(1)}, bf16[1,256,2048]{2,1,0:T(8,128)(2,1)}, u32[]{:S(2)}) copy-start(bf16[1,256,2048]{2,1,0:T(8,128)(2,1)} %param.8) | copy-start | bytes 3145732
  285.2 164.2 %reduce-scatter.5.cloned.1.call-start = ((), (), s32[]{:S(2)}) async-start(), calls=%async_computation.5 | async-start | bytes 2359296 | tf_op jit(solution)/shard_map/reduce_scatter | solution.py:23
  452.3 17.7 %all-to-all-start.1 = ((f32[16,6,1,2048]{3,2,1,0:T(1,128)}), f32[16,6,1,2048]{3,2,1,0:T(1,128)S(1)}, u32[]{:S(2)}, u32[]{:S(2)}) async-start(f32[16,6,1,2048]{3,2,1,0:T(1,128)} %copy.23), calls=%async_computation.3 | async-start | bytes 1572864 | tf_op jit(solution)/shard_map/all_to_all | solution.py:91
Sparse Core Ops, SparseCore 0:
  285.3 130.2 reduce-scatter.2
  418.1 31.2 reduce-scatter.4
